TPU v7x, 256 devices: a 2x2x32 block of a 4x8x32 slice. The times are simulated.
256 devices in a mesh: station: 4 (over x, y), tm: 64 (over z, core).
Axes of the slice: x: 2, y: 2, z: 32, core: 2. Of those that a mesh axis runs over, the one named last changes fastest.
The devices are a block of a 4x8x32 slice.
Arguments:
- spectra: float32 [512, 8, 16384], P('tm', 'station'), parts along dimension 1, may hold values from -6 to 6
- synth_taps: float32 [16, 512], replicated, may hold values from -1.5 to 1.5
- analysis_taps: float32 [16, 512], replicated, may hold values from -1.5 to 1.5
Outputs:
- channels: float32 [512, 8, 20480], P('tm', 'station'), parts along dimension 1
There are 4 independent parts, one for each index of `station`. A program takes and returns all parts, laid end to end along the dimension named above; an argument that names none is the same for every part. Nothing has to cross between parts.
All inputs are finite; a program needn't handle non-finite values.
Results may differ from a plain program's by a relative error of at most 0.00007.
Values sent between devices are 32-bit elements; how exact they have to be, the bound alone decides.
A program may use at most 64 MiB of HBM per device.

v0:
```python
import math

import jax
import jax.numpy as jnp
from jax import lax
from jax.sharding import PartitionSpec as P

M = 512
RT = 32
PHASES = 64


def passed_along(value, axis, by):
    count = lax.axis_size(axis)
    pairs = [(i, i + by) for i in range(count) if 0 <= i + by < count]
    return lax.ppermute(value, axis, pairs)


def tables(width):
    index = jnp.arange(width, dtype=jnp.int32)
    product = index[:, None] * index[None, :] % width
    angle = product.astype(jnp.float32) * (2.0 * math.pi / width)
    scale = 1.0 / math.sqrt(width)
    return (jnp.cos(angle) * scale, jnp.sin(angle) * scale)


def resampler(width, taps_len, phases):
    out_width = 5 * width // 4
    sample = jnp.arange(out_width, dtype=jnp.int32)[:, None]
    column = jnp.arange(2 * width, dtype=jnp.int32)[None, :]
    start = 4 * sample // 5
    phase = phases * (4 * sample % 5) // 5
    lag = start + width - column
    offset = lag.astype(jnp.float32) + phase.astype(jnp.float32) / phases - (taps_len // 2 - 1)
    window = 0.5 + 0.5 * jnp.cos(math.pi * offset / (taps_len / 2.0))
    coeff = 0.9 * jnp.sinc(0.9 * offset) * window
    valid = (lag >= 0) & (lag < taps_len)
    full = jnp.where(valid, coeff, jnp.zeros_like(coeff))
    return (full[:, width:], full[:, :width])


def inverse(raw, cosines, sines):
    dims = (((0,), (0,)), ((), ()))
    with_cos = lax.dot_general(
        raw, cosines, dims, precision=lax.Precision.HIGHEST, preferred_element_type=jnp.float32
    )
    with_sin = lax.dot_general(
        raw, sines, dims, precision=lax.Precision.HIGHEST, preferred_element_type=jnp.float32
    )
    return jnp.stack([with_cos[0] - with_sin[1], with_sin[0] + with_cos[1]])


def forward(frames, cosines, sines):
    dims = (((1,), (2,)), ((), ()))
    with_cos = lax.dot_general(
        cosines, frames, dims, precision=lax.Precision.HIGHEST, preferred_element_type=jnp.float32
    )
    with_sin = lax.dot_general(
        sines, frames, dims, precision=lax.Precision.HIGHEST, preferred_element_type=jnp.float32
    )
    return jnp.stack([with_cos[:, 0] + with_sin[:, 1], with_cos[:, 1] - with_sin[:, 0]], axis=1)


def filtered(frames, taps):
    count = frames.shape[1] - taps.shape[0] + 1
    total = jnp.zeros((2, count, frames.shape[2]), jnp.float32)
    for lag_index in range(taps.shape[0]):
        first = taps.shape[0] - 1 - lag_index
        total = total + taps[lag_index][None, None, :] * frames[:, first : first + count]
    return total


def resample(stream, current, previous):
    width = stream.shape[2]
    now_rows = stream[:, 1:].reshape(-1, width)
    before_rows = stream[:, :-1].reshape(-1, width)
    dims = (((1,), (1,)), ((), ()))
    out = lax.dot_general(
        now_rows, current, dims, precision=lax.Precision.HIGHEST, preferred_element_type=jnp.float32
    )
    out = out + lax.dot_general(
        before_rows,
        previous,
        dims,
        precision=lax.Precision.HIGHEST,
        preferred_element_type=jnp.float32,
    )
    return out.reshape(2, -1, width)


def shards(spectra, synth_taps, analysis_taps):
    cosines, sines = tables(M)
    current, previous = resampler(M, RT, PHASES)
    branch_taps = synth_taps.shape[0]
    blocks = spectra.reshape(spectra.shape[0], 2, lax.axis_size("tm"), -1)
    spread = inverse(
        lax.all_to_all(blocks, "tm", split_axis=2, concat_axis=0, tiled=True)[:, :, 0, :],
        cosines,
        sines,
    )
    own_frames = spread.shape[1]
    earlier = passed_along(spread[:, own_frames - branch_taps :], "tm", 1)
    stream = filtered(jnp.concatenate([earlier, spread], axis=1), synth_taps)
    resampled = resample(stream, current, previous)
    kept = resampled.shape[1]
    carried = passed_along(resampled[:, kept - (branch_taps - 1) :], "tm", 1)
    resampled = jnp.concatenate([carried, resampled], axis=1)
    windowed = filtered(resampled, analysis_taps)
    spectrum = forward(windowed, cosines, sines)
    return lax.all_to_all(spectrum, "tm", split_axis=0, concat_axis=2, tiled=True)


def solution(mesh):
    in_specs = (P("tm", "station", None), P(), P())
    out_specs = P("tm", "station", None)
    return jax.shard_map(shards, mesh=mesh, in_specs=in_specs, out_specs=out_specs, check_vma=False)
```

profile of v0, /device:TPU:37, one launch (start us, length us, event | category | flops | bytes accessed | tf_op | source)
XLA Modules:
  0.0 367.4 jit_solution(11203837430081772985)
XLA Ops:
  0.0 2.1 reshape.107
  2.1 1.6 copy.17
  3.7 34.5 %all-to-all-start = ((f32[8,2,64,256]{3,0,1,2:T(8,128)}), f32[8,2,64,256]{3,0,1,2:T(8,128)}, u32[]{:S(2)}, u32[]{:S(2)}) async-start(f32[8,2,64,256]{3,0,1,2:T(8,128)} %copy.17), calls=%async_computation | async-start | bytes 2097152 | tf_op jit(solution)/shard_map/all_to_all | solution.py:97
  38.3 12.8 %multiply_select_fusion = f32[640,1024]{1,0:T(8,128)S(1)} fusion(f32[640]{0:T(1024)S(1)} %fusion.104, s32[640]{0:T(1024)S(1)} %fusion.101), kind=kLoop, calls=%fused_computation.27 | loop fusion | flops 30801920 | bytes 2626560 | tf_op jit(solution)/shard_map/jit(_where)/select_n | solution.py:38
  51.0 94.5 %all-to-all-done = f32[8,2,64,256]{3,0,1,2:T(8,128)} async-done(((f32[8,2,64,256]{3,0,1,2:T(8,128)}), f32[8,2,64,256]{3,0,1,2:T(8,128)}, u32[]{:S(2)}, u32[]{:S(2)}) %all-to-all-start) | async-done | bytes 1048608 | tf_op jit(solution)/shard_map/all_to_all | solution.py:97
  145.6 8.6 %convolution_bitcast_fusion = f32[2,256,512]{2,1,0:T(8,128)S(1)} fusion(f32[8,2,64,256]{3,0,1,2:T(8,128)} %all-to-all-done), kind=kOutput, calls=%fused_computation.47 | convolution fusion | flops 1614544896 | bytes 2097152 | tf_op jit(solution)/shard_map/dot_general | solution.py:47
  154.1 8.5 %convolution_bitcast_fusion.1 = f32[2,256,512]{2,1,0:T(8,128)S(1)} fusion(f32[8,2,64,256]{3,0,1,2:T(8,128)} %all-to-all-done), kind=kOutput, calls=%fused_computation.48 | convolution fusion | flops 1614544896 | bytes 2097152 | tf_op jit(solution)/shard_map/dot_general | solution.py:44
  162.7 0.0 copy-start
  162.7 0.2 slice_subtract_fusion.1
  162.9 4.4 %collective-permute-start = (f32[2,16,512]{2,1,0:T(8,128)S(1)}, f32[2,16,512]{2,1,0:T(8,128)S(1)}, u32[]{:S(2)}, u32[]{:S(2)}) collective-permute-start(f32[2,16,512]{2,1,0:T(8,128)S(1)} %pad_maximum_fusion.2), channel_id=1, source_target_pairs={{0,1},{1,2},{2,3},{3,4},{4,5},{5,6},{6,7},{7,8},{8,9},{9,10},{10,1... | collective-permute-start | bytes 196616 | tf_op jit(solution)/shard_map/ppermute | solution.py:16
  167.3 0.0 copy-done
  167.4 1.3 collective-permute-done
  168.6 0.1 maximum_maximum_fusion
  168.7 2.5 fusion.62
  171.3 0.2 fusion.131
  171.5 2.7 fusion.60
  174.2 3.8 %convolution_add_fusion = f32[512,640]{1,0:T(8,128)} fusion(f32[512,640]{1,0:T(8,128)S(1)} %fusion.60, f32[512,512]{1,0:T(8,128)S(1)} %bitcast.69, f32[640,1024]{1,0:T(8,128)S(1)} %multiply_select_fusion), kind=kOutput, calls=%fused_computation.46 | convolution fusion | flops 2013593600 | bytes 4980736 | tf_op jit(solution)/shard_map/dot_general | solution.py:81
  178.1 0.0 copy-start.1
  178.1 1.6 reshape.104
  179.7 4.3 %collective-permute-start.1 = (f32[2,15,512]{2,1,0:T(8,128)S(1)}, f32[2,15,512]{2,1,0:T(8,128)S(1)}, u32[]{:S(2)}, u32[]{:S(2)}) collective-permute-start(f32[2,15,512]{2,1,0:T(8,128)S(1)} %slice.332), channel_id=1, source_target_pairs={{0,1},{1,2},{2,3},{3,4},{4,5},{5,6},{6,7},{7,8},{8,9},{9,10},{10,1... | collective-permute-start | bytes 184328 | tf_op jit(solution)/shard_map/ppermute | solution.py:16
  184.0 0.0 copy-done.1
  184.0 1.3 collective-permute-done.1
  185.3 2.8 fusion.18
  188.0 6.9 %fusion.82 = f32[512,2,320]{0,2,1:T(8,128)S(1)} fusion(f32[2,320,512]{2,1,0:T(8,128)S(1)} %fusion.18), kind=kOutput, calls=%fused_computation.147 | convolution fusion | flops 2017198080 | bytes 2621440 | tf_op jit(solution)/shard_map/dot_general | solution.py:58
  194.9 6.9 %fusion.85 = f32[512,2,320]{0,2,1:T(8,128)S(1)} fusion(f32[2,320,512]{2,1,0:T(8,128)S(1)} %fusion.18), kind=kOutput, calls=%fused_computation.150 | convolution fusion | flops 2017198080 | bytes 2621440 | tf_op jit(solution)/shard_map/dot_general | solution.py:55
  201.8 0.3 slice_add_fusion
  202.1 0.1 pad_maximum_fusion.1
  202.2 1.2 copy.21
  203.4 161.1 %all_to_all.33 = f32[512,2,320]{2,1,0:T(2,128)S(1)} all-to-all(f32[512,2,320]{2,1,0:T(2,128)S(1)} %copy.21), channel_id=1, replica_groups=mesh['station'=4,'tm'=64] {'tm'}, dimensions={0} | all-to-all | bytes 2621440 | tf_op jit(solution)/shard_map/all_to_all | solution.py:110
  364.5 0.1 copy.40
  364.6 0.3 copy.29
  364.9 2.3 reshape.108
  (6 shorter events, 0.1 us)
Async XLA Ops:
  3.7 141.9 %all-to-all-start = ((f32[8,2,64,256]{3,0,1,2:T(8,128)}), f32[8,2,64,256]{3,0,1,2:T(8,128)}, u32[]{:S(2)}, u32[]{:S(2)}) async-start(f32[8,2,64,256]{3,0,1,2:T(8,128)} %copy.17), calls=%async_computation | async-start | bytes 2097152 | tf_op jit(solution)/shard_map/all_to_all | solution.py:97
  162.7 4.6 %copy-start = (f32[16,512]{1,0:T(8,128)S(1)}, f32[16,512]{1,0:T(8,128)}, u32[]{:S(2)}) copy-start(f32[16,512]{1,0:T(8,128)} %param.4) | copy-start | bytes 98308
  162.9 5.7 %collective-permute-start = (f32[2,16,512]{2,1,0:T(8,128)S(1)}, f32[2,16,512]{2,1,0:T(8,128)S(1)}, u32[]{:S(2)}, u32[]{:S(2)}) collective-permute-start(f32[2,16,512]{2,1,0:T(8,128)S(1)} %pad_maximum_fusion.2), channel_id=1, source_target_pairs={{0,1},{1,2},{2,3},{3,4},{4,5},{5,6},{6,7},{7,8},{8,9},{9,10},{10,1... | collective-permute-start | bytes 196616 | tf_op jit(solution)/shard_map/ppermute | solution.py:16
  178.1 5.9 %copy-start.1 = (f32[16,512]{1,0:T(8,128)S(1)}, f32[16,512]{1,0:T(8,128)}, u32[]{:S(2)}) copy-start(f32[16,512]{1,0:T(8,128)} %param.5) | copy-start | bytes 98308
  179.7 5.6 %collective-permute-start.1 = (f32[2,15,512]{2,1,0:T(8,128)S(1)}, f32[2,15,512]{2,1,0:T(8,128)S(1)}, u32[]{:S(2)}, u32[]{:S(2)}) collective-permute-start(f32[2,15,512]{2,1,0:T(8,128)S(1)} %slice.332), channel_id=1, source_target_pairs={{0,1},{1,2},{2,3},{3,4},{4,5},{5,6},{6,7},{7,8},{8,9},{9,10},{10,1... | collective-permute-start | bytes 184328 | tf_op jit(solution)/shard_map/ppermute | solution.py:16
where the time goes:
time: 372 us; the launch traced here: 367 us
  blocking collectives  161 us (43%)
  waiting for transfers between devices  97.1 us (26%)
  starting transfers between devices  43.2 us (12%)
  matrix products  37.4 us (10%)
  other arithmetic  18.8 us (5%)
  local copies, waits for them, and re-layouts  9.47 us (3%)
    all_to_all x1, blocking collectives, shards(): lax.all_to_all(spectrum, 'tm', split_axis=0, concat_axis=2, tiled=True)  161 us
    all_to_all x1, waiting for transfers between devices, shards(): lax.all_to_all(blocks, 'tm', split_axis=2, concat_axis=0, tiled=True)  94.5 us
    all_to_all x1, starting transfers between devices, shards(): lax.all_to_all(blocks, 'tm', split_axis=2, concat_axis=0, tiled=True)  34.5 us
    select_n x1, other arithmetic, resampler(): full = jnp.where(valid, coeff, jnp.zeros_like(coeff))  12.8 us
    ppermute x2, starting transfers between devices, passed_along(): return lax.ppermute(value, axis, pairs)  8.68 us
    dot_general x1, matrix products, inverse(): lax.dot_general(raw, sines, dims, precision=lax.Precision.HIGHEST, prefer...  8.57 us
    dot_general x1, matrix products, inverse(): lax.dot_general(raw, cosines, dims, precision=lax.Precision.HIGHEST, pref...  8.54 us
  transfers between devices with their start and end apart: 3, of which 3 were waited for; matrix products, arithmetic and copies ran while one was open for 3% of the time, Pallas kernels for 0%

commit v1 on v0

v1 whole, which is shorter than its diff:
```python
import functools
import math

import jax
import jax.numpy as jnp
import numpy as np
from jax import lax
from jax.experimental import pallas as pl
from jax.experimental.pallas import tpu as pltpu
from jax.sharding import PartitionSpec as P

RT = 32
PHASES = 64
UP, DOWN = 5, 4
W = 64
L = 128
HALO = 32
BACK = 16
MESH = pl.DeviceIdType.MESH
F32 = jnp.float32


def split(a):
    hi = a.astype(jnp.bfloat16)
    return hi, (a - hi.astype(F32)).astype(jnp.bfloat16)


def dft_table(width):
    k = np.outer(np.arange(width), np.arange(width)) % width
    angle = k * (2.0 * math.pi / width)
    both = np.concatenate([np.cos(angle), np.sin(angle)], axis=1) / math.sqrt(width)
    return both.astype(np.float32)


def resample_table(width):
    out_width = UP * width // DOWN
    sample = np.arange(out_width)[None, :]
    row = np.arange(L + width)[:, None]
    lag = DOWN * sample // UP + L - row
    phase = PHASES * (DOWN * sample % UP) // UP
    t = lag + phase / PHASES - (RT // 2 - 1)
    coeff = 0.9 * np.sinc(0.9 * t) * (0.5 + 0.5 * np.cos(math.pi * t / (RT / 2.0)))
    return np.where((lag >= 0) & (lag < RT), coeff, 0.0).astype(np.float32)


def halves(table):
    hi = table.astype(jnp.bfloat16)
    lo = (table - hi.astype(np.float32)).astype(jnp.bfloat16)
    return jnp.asarray(np.stack([hi, lo]))


def product(a, b, dims):
    (ah, al), (bh, bl) = a, b
    dot = lambda x, y: lax.dot_general(x, y, (dims, ((), ())), preferred_element_type=F32)
    return dot(ah, bh) + (dot(ah, bl) + dot(al, bh))


def kernel(
    n, x_ref, st_ref, at_ref, cs_hbm, rs_hbm, o_ref,
    cs, rs, xs, land1, v_all, hbuf, vwin, ywin, zst, zfull, zwin, u2, sbuf, land2,
    csem, rsem, send1, recv1, hsend, hrecv, send2, recv2,
):
    me = lax.axis_index("tm")
    station = lax.axis_index("station")
    nc = n // 2
    chip, core = me // 2, me % 2
    taps = st_ref.shape[0]
    m = st_ref.shape[1]
    chunks = land1.shape[0]
    pieces = land2.shape[0]
    cb = x_ref.shape[1]
    blocks = m // L

    barrier = pltpu.get_barrier_semaphore()

    def greet(j, c):
        pl.semaphore_signal(barrier, inc=1, device_id=(station, (me + j) % n), device_id_type=MESH)
        return c

    lax.fori_loop(1, n, greet, 0)
    get_cs = pltpu.make_async_copy(cs_hbm, cs, csem)
    get_rs = pltpu.make_async_copy(rs_hbm, rs, rsem)
    get_cs.start()
    get_rs.start()

    low = lax.broadcasted_iota(jnp.int32, (cb, L), 1) < W

    def arrange(t, c):
        a = x_ref[0, :, pl.ds(pl.multiple_of(t * L, L), L)]
        b = x_ref[1, :, pl.ds(pl.multiple_of(t * L, L), L)]
        xs[2 * t] = jnp.where(low, a, pltpu.roll(b, W, 1))
        xs[2 * t + 1] = jnp.where(low, pltpu.roll(a, W, 1), b)
        return c

    lax.fori_loop(0, n * chunks // 2, arrange, 0)
    ywin[:, 0:8, :] = jnp.zeros((2, 8, m), F32)
    pl.semaphore_wait(barrier, n - 1)

    def send_to_all(source, target, sent, got):
        def send(dev):
            pltpu.make_async_remote_copy(
                src_ref=source(dev), dst_ref=target, send_sem=sent, recv_sem=got,
                device_id=(station, dev), device_id_type=MESH,
            ).start()

        def step(j, c):
            jj = j // 2
            d = nc // 2 - jj // 2
            sign = 1 - 2 * (jj % 2)
            dev = ((chip + sign * d + nc) % nc) * 2 + (j % 2 + core) % 2

            @pl.when(jnp.logical_not(jnp.logical_and(2 * d == nc, sign == -1)))
            def _():
                send(dev)

            return c

        lax.fori_loop(0, 2 * nc, step, 0)
        send(chip * 2 + 1 - core)

    def wait_bytes(ref, sem):
        part = ref.at[pl.ds(0, n - 1)]
        pltpu.make_async_copy(part, part, sem).wait()

    def send_in(k):
        send_to_all(lambda dev: xs.at[dev * chunks + k], land1.at[k, me], send1.at[k], recv1.at[k])
        land1[k, me] = xs[me * chunks + k]

    def synthesize(k):
        wait_bytes(land1.at[k], recv1.at[k])
        raw = land1[k].reshape(m, L)
        out = product(split(raw.T), (cs[0], cs[1]), ((1,), (0,)))
        v_all[k, 0] = out[:W, :m] - out[W:, m:]
        v_all[k, 1] = out[:W, m:] + out[W:, :m]

    last = chunks - 1
    send_in(last)
    send_in(0)
    get_cs.wait()
    synthesize(last)
    tail = pltpu.make_async_remote_copy(
        src_ref=v_all.at[last, :, pl.ds(W - HALO, HALO)], dst_ref=hbuf,
        send_sem=hsend, recv_sem=hrecv,
        device_id=(station, (me + 1) % n), device_id_type=MESH,
    )

    @pl.when(me < n - 1)
    def _():
        tail.start()

    def send_rest(k, c):
        send_in(k)
        return c

    lax.fori_loop(1, last, send_rest, 0)
    get_rs.wait()

    def resampled(k):
        @pl.when(k == 0)
        def _():
            @pl.when(me == 0)
            def _():
                vwin[:, 0:HALO, :] = jnp.zeros((2, HALO, m), F32)

            @pl.when(me > 0)
            def _():
                tail.wait_recv()
                vwin[:, 0:HALO, :] = hbuf[...]

        @pl.when(k > 0)
        def _():
            vwin[:, 0:HALO, :] = vwin[:, W : W + HALO, :]

        vwin[:, HALO:, :] = v_all[k]
        rows = BACK + W
        for ri in range(2):
            for b in range(blocks):
                lanes = pl.ds(b * L, L)
                total = jnp.zeros((rows, L), F32)
                for p in range(taps):
                    total = total + st_ref[p : p + 1, lanes] * vwin[ri, pl.ds(BACK - p, rows), lanes]
                ywin[ri, pl.ds(8, rows), lanes] = total
        left = jnp.concatenate(
            [
                jnp.concatenate([ywin[ri, pl.ds(7, rows), pl.ds(m - L, L)], ywin[ri, pl.ds(8, rows), :]], axis=1)
                for ri in range(2)
            ],
            axis=0,
        )
        out = product(split(left), (rs[0], rs[1]), ((1,), (0,)))
        wide = UP * blocks // DOWN
        for ri in range(2):
            for j in range(wide):
                zst[ri, pl.ds(j, rows, stride=wide), :] = out[ri * rows : (ri + 1) * rows, j * L : (j + 1) * L]

        @pl.when(k == 0)
        def _():
            zfull[:, 0 : BACK * wide, :] = zst[:, 0 : BACK * wide, :]

        zfull[:, pl.ds(pl.multiple_of(BACK * wide + k * (W * wide), 8), W * wide), :] = zst[:, BACK * wide :, :]

    def analyzed(p):
        wide = UP * blocks // DOWN
        first = BACK * wide - BACK * blocks
        zwin[...] = zfull[:, pl.ds(pl.multiple_of(first + p * (W * blocks), 8), (BACK + W) * blocks), :]
        for b in range(blocks):
            for ri in range(2):
                total = jnp.zeros((W, L), F32)
                for t in range(taps):
                    total = total + at_ref[t : t + 1, pl.ds(b * L, L)] * zwin[
                        ri, pl.ds((BACK - t) * blocks + b, W, stride=blocks), :
                    ]
                if ri == 0:
                    u2[0:W, pl.ds(b * L, L)] = total
                    u2[W:, pl.ds(m + b * L, L)] = -total
                else:
                    u2[0:W, pl.ds(m + b * L, L)] = total
                    u2[W:, pl.ds(b * L, L)] = total
        out = product((cs[0], cs[1]), split(u2[...]), ((1,), (1,)))
        sbuf[p] = out.reshape(n, cb, L)
        land2[p, me] = sbuf[p, me]
        send_to_all(lambda dev: sbuf.at[p, dev], land2.at[p, me], send2.at[p], recv2.at[p])

    def step(p, c):
        @pl.when(p < last)
        def _():
            synthesize(p)

        @pl.when(p < chunks)
        def _():
            resampled(p)

        analyzed(p)
        return c

    lax.fori_loop(0, pieces, step, 0)

    @pl.when(me < n - 1)
    def _():
        tail.wait_send()

    for k in range(chunks):
        wait_bytes(land1.at[k], send1.at[k])
    for p in range(pieces):
        wait_bytes(land2.at[p], recv2.at[p])

    def place(t, c):
        for u in range(pieces):
            a = land2[(2 * u) % pieces, 2 * t + (2 * u) // pieces]
            b = land2[(2 * u + 1) % pieces, 2 * t + (2 * u + 1) // pieces]
            lanes = pl.ds(pl.multiple_of(t * (pieces * L) + u * L, L), L)
            o_ref[0, :, lanes] = jnp.where(low, a, pltpu.roll(b, W, 1))
            o_ref[1, :, lanes] = jnp.where(low, pltpu.roll(a, W, 1), b)
        return c

    lax.fori_loop(0, n // 2, place, 0)
    for p in range(pieces):
        wait_bytes(land2.at[p], send2.at[p])


def shards(n, spectra, synth_taps, analysis_taps):
    cb, _, frames = spectra.shape
    m = synth_taps.shape[1]
    own = frames // n
    chunks = own // W
    pieces = UP * own // DOWN // W
    wide = UP * m // DOWN // L
    blocks = m // L
    vmem = pl.BlockSpec(memory_space=pltpu.VMEM)
    hbm = pl.BlockSpec(memory_space=pl.ANY)
    dma = pltpu.SemaphoreType.DMA
    out = pl.pallas_call(
        functools.partial(kernel, n),
        out_shape=jax.ShapeDtypeStruct((2, cb, UP * frames // DOWN), F32),
        in_specs=[vmem, vmem, vmem, hbm, hbm],
        out_specs=vmem,
        scratch_shapes=[
            pltpu.VMEM((2, m, 2 * m), jnp.bfloat16),
            pltpu.VMEM((2, m + L, wide * L), jnp.bfloat16),
            pltpu.VMEM((n * chunks, cb, L), F32),
            pltpu.VMEM((chunks, n, cb, L), F32),
            pltpu.VMEM((chunks, 2, W, m), F32),
            pltpu.VMEM((2, HALO, m), F32),
            pltpu.VMEM((2, HALO + W, m), F32),
            pltpu.VMEM((2, 8 + BACK + W, m), F32),
            pltpu.VMEM((2, (BACK + W) * wide, L), F32),
            pltpu.VMEM((2, (BACK + own) * wide, L), F32),
            pltpu.VMEM((2, (BACK + W) * blocks, L), F32),
            pltpu.VMEM((2 * W, 2 * m), F32),
            pltpu.VMEM((pieces, n, cb, L), F32),
            pltpu.VMEM((pieces, n, cb, L), F32),
            dma, dma, dma((chunks,)), dma((chunks,)), dma, dma, dma((pieces,)), dma((pieces,)),
        ],
        compiler_params=pltpu.CompilerParams(
            collective_id=0, has_side_effects=True, vmem_limit_bytes=40 << 20
        ),
    )(
        jnp.swapaxes(spectra, 0, 1), synth_taps, analysis_taps,
        halves(dft_table(m)), halves(resample_table(m)),
    )
    return jnp.swapaxes(out, 0, 1)


def solution(mesh):
    in_specs = (P("tm", "station", None), P(), P())
    out_specs = P("tm", "station", None)
    body = functools.partial(shards, mesh.shape["tm"])
    return jax.shard_map(body, mesh=mesh, in_specs=in_specs, out_specs=out_specs, check_vma=False)
```

time: 372 us -> 250 us (0.67); the launches traced: 367 us -> 250 us
  Pallas kernels: 0 us -> 243 us
  blocking collectives: 161 us -> 0 us
  waiting for transfers between devices: 97.1 us -> 0 us
  starting transfers between devices: 43.2 us -> 0 us
  matrix products: 37.4 us -> 0 us
  other arithmetic: 18.8 us -> 0 us
    pallas_call x0 -> x1, Pallas kernels: none -> 243 us  [shards(): pl.pallas_call(functools.partial(kernel, n), out_shape=jax.ShapeDtypeStru...]
    all_to_all x1 -> x0, blocking collectives: 161 us -> none  [shards(): lax.all_to_all(spectrum, 'tm', split_axis=0, concat_axis=2, tiled=True)]
    all_to_all x1 -> x0, waiting for transfers between devices: 94.5 us -> none  [shards(): lax.all_to_all(blocks, 'tm', split_axis=2, concat_axis=0, tiled=True)]
    dot_general x6 -> x0, matrix products: 37.4 us -> none  [the longest x1 8.57 us: inverse(): lax.dot_general(raw, sines, dims, precision=lax.Precision.HIGHEST, prefer...]
    all_to_all x1 -> x0, starting transfers between devices: 34.5 us -> none  [shards(): lax.all_to_all(blocks, 'tm', split_axis=2, concat_axis=0, tiled=True)]
    select_n x1 -> x0, other arithmetic: 12.8 us -> none  [resampler(): full = jnp.where(valid, coeff, jnp.zeros_like(coeff))]
    ppermute x2 -> x0, starting transfers between devices: 8.68 us -> none  [passed_along(): return lax.ppermute(value, axis, pairs)]
    add x4 -> x0, other arithmetic: 5.6 us -> none  [the longest x2 5.31 us: filtered(): total + taps[lag_index][None, None, :] * frames[:, first:first + count]]
  transfers between devices with their start and end apart: 3 -> 0, of which waited for: 3 -> 0; matrix products, arithmetic and copies ran while one was open for 3% -> 0% of each run, Pallas kernels for 0% -> 0%
where the time goes in v1:
time: 250 us
  Pallas kernels  243 us (97%)
  local copies, waits for them, and re-layouts  7 us (3%)
    pallas_call x1, Pallas kernels, shards(): pl.pallas_call(functools.partial(kernel, n), out_shape=jax.ShapeDtypeStru...  243 us

profile of v1, /device:TPU:37, one launch (start us, length us, event | category | flops | bytes accessed | tf_op | source)
XLA Modules:
  0.0 249.8 jit_solution(1777773877473124599)
XLA Ops:
  0.0 0.0 copy-start
  0.0 2.0 copy.9
  2.0 0.0 copy-done
  2.0 0.0 copy-start.1
  2.0 1.4 copy-done.1
  3.4 0.0 copy-start.2
  3.4 0.8 copy-done.2
  4.2 0.0 copy-start.3
  4.2 0.8 copy-done.3
  5.0 242.8 %shard_map.55 = f32[2,8,20480]{2,1,0:T(8,128)S(1)} custom-call(f32[2,8,16384]{2,1,0:T(8,128)S(1)} %bitcast.5, f32[16,512]{1,0:T(8,128)S(1)} %copy-done.2, f32[16,512]{1,0:T(8,128)S(1)} %copy-done.3, bf16[2,512,1024]{2,1,0:T(8,128)(2,1)S(1)} %copy-done, bf16[2,640,640]{2,1,0:T(8,128)(2,1)S(1)} %copy-done.1), custom_call_target="tpu_custom_call" | custom-call | tf_op jit(solution)/shard_map/pallas_call | solution.py:272
  247.8 2.1 copy.7
Async XLA Ops:
  0.0 2.0 copy-start
  2.0 1.4 copy-start.1
  3.4 0.8 copy-start.2
  4.2 0.8 copy-start.3

commit v2 on v1

--- a/solution.py
+++ b/solution.py
@@ -12,6 +12,7 @@
 RT = 32
 PHASES = 64
 UP, DOWN = 5, 4
+REACH = 4
 W = 64
 L = 128
 HALO = 32
@@ -56,9 +57,9 @@
 
 
 def kernel(
-    n, x_ref, st_ref, at_ref, cs_hbm, rs_hbm, o_ref,
-    cs, rs, xs, land1, v_all, hbuf, vwin, ywin, zst, zfull, zwin, u2, sbuf, land2,
-    csem, rsem, send1, recv1, hsend, hrecv, send2, recv2,
+    n, x_hbm, st_hbm, at_hbm, cs_hbm, rs_hbm, o_ref,
+    x_ref, st_ref, at_ref, cs, rs, xs, land1, v_all, hbuf, vwin, ywin, zst, zfull, zwin, u2, sbuf, land2,
+    xsem, ssem, asem, csem, rsem, send1, recv1, hsend, hrecv, send2, recv2, ready,
 ):
     me = lax.axis_index("tm")
     station = lax.axis_index("station")
@@ -68,35 +69,54 @@
     m = st_ref.shape[1]
     chunks = land1.shape[0]
     pieces = land2.shape[0]
-    cb = x_ref.shape[1]
+    cb = xs.shape[1]
+    out_rows = o_ref.shape[0] // cb
     blocks = m // L
 
+    def at(offset, c):
+        return (chip + offset + nc) % nc * 2 + c
+
+    def signal(sem, dev):
+        pl.semaphore_signal(sem, inc=1, device_id=(station, dev), device_id_type=MESH)
+
     barrier = pltpu.get_barrier_semaphore()
-
-    def greet(j, c):
-        pl.semaphore_signal(barrier, inc=1, device_id=(station, (me + j) % n), device_id_type=MESH)
-        return c
-
-    lax.fori_loop(1, n, greet, 0)
+    half = nc // 2
+    reach = min(REACH, half)
+    met = 1
+    signal(barrier, at(0, 1 - core))
+    for d in range(1, reach + 1):
+        for offset in (d,) if 2 * d == nc else (d, -d):
+            for c in range(2):
+                signal(barrier, at(offset, c))
+                met += 1
+    in_rows = x_hbm.shape[0] // cb
+    pitch = x_ref.shape[0] // cb
+    get_x = [
+        pltpu.make_async_copy(
+            x_hbm.at[pl.ds(i * in_rows, in_rows)], x_ref.at[pl.ds(i * pitch, in_rows)], xsem.at[i]
+        )
+        for i in range(cb)
+    ]
+    for copy in get_x:
+        copy.start()
     get_cs = pltpu.make_async_copy(cs_hbm, cs, csem)
     get_rs = pltpu.make_async_copy(rs_hbm, rs, rsem)
-    get_cs.start()
-    get_rs.start()
+    get_st = pltpu.make_async_copy(st_hbm, st_ref, ssem)
+    get_at = pltpu.make_async_copy(at_hbm, at_ref, asem)
+    for copy in (get_cs, get_rs, get_st, get_at):
+        copy.start()
 
     low = lax.broadcasted_iota(jnp.int32, (cb, L), 1) < W
 
-    def arrange(t, c):
-        a = x_ref[0, :, pl.ds(pl.multiple_of(t * L, L), L)]
-        b = x_ref[1, :, pl.ds(pl.multiple_of(t * L, L), L)]
-        xs[2 * t] = jnp.where(low, a, pltpu.roll(b, W, 1))
-        xs[2 * t + 1] = jnp.where(low, pltpu.roll(a, W, 1), b)
+    def arrange(i, c):
+        for t in [chunks * i + j for j in range(chunks)]:
+            a = x_ref[pl.ds(2 * t, cb, stride=pitch), :]
+            b = x_ref[pl.ds(2 * t + 1, cb, stride=pitch), :]
+            xs[2 * t] = jnp.where(low, a, pltpu.roll(b, W, 1))
+            xs[2 * t + 1] = jnp.where(low, pltpu.roll(a, W, 1), b)
         return c
 
-    lax.fori_loop(0, n * chunks // 2, arrange, 0)
-    ywin[:, 0:8, :] = jnp.zeros((2, 8, m), F32)
-    pl.semaphore_wait(barrier, n - 1)
-
-    def send_to_all(source, target, sent, got):
+    def send_to(source, target, sent, got, near, far):
         def send(dev):
             pltpu.make_async_remote_copy(
                 src_ref=source(dev), dst_ref=target, send_sem=sent, recv_sem=got,
@@ -104,27 +124,25 @@
             ).start()
 
         def step(j, c):
-            jj = j // 2
-            d = nc // 2 - jj // 2
-            sign = 1 - 2 * (jj % 2)
-            dev = ((chip + sign * d + nc) % nc) * 2 + (j % 2 + core) % 2
+            d = far - j // 4
+            sign = 1 - 2 * (j // 2 % 2)
 
             @pl.when(jnp.logical_not(jnp.logical_and(2 * d == nc, sign == -1)))
             def _():
-                send(dev)
+                send(at(sign * d, (j + core) % 2))
 
             return c
 
-        lax.fori_loop(0, 2 * nc, step, 0)
-        send(chip * 2 + 1 - core)
+        lax.fori_loop(0, 4 * (far - near + 1), step, 0)
+        if near == 1:
+            send(at(0, 1 - core))
+
+    def send_in(k, near, far):
+        send_to(lambda dev: xs.at[dev * chunks + k], land1.at[k, me], send1.at[k], recv1.at[k], near, far)
 
     def wait_bytes(ref, sem):
         part = ref.at[pl.ds(0, n - 1)]
         pltpu.make_async_copy(part, part, sem).wait()
-
-    def send_in(k):
-        send_to_all(lambda dev: xs.at[dev * chunks + k], land1.at[k, me], send1.at[k], recv1.at[k])
-        land1[k, me] = xs[me * chunks + k]
 
     def synthesize(k):
         wait_bytes(land1.at[k], recv1.at[k])
@@ -134,8 +152,24 @@
         v_all[k, 1] = out[:W, m:] + out[W:, :m]
 
     last = chunks - 1
-    send_in(last)
-    send_in(0)
+    for copy in get_x:
+        copy.wait()
+    lax.fori_loop(0, n // 2, arrange, 0)
+    pl.semaphore_wait(barrier, met)
+    known, turn, done = reach, 0, 0
+    while known < half:
+        for offset in (known, -known):
+            signal(ready.at[turn], at(offset, core))
+        for k in range(chunks):
+            send_in((k - 1) % chunks, done + 1, known)
+        done = known
+        pl.semaphore_wait(ready.at[turn], 2)
+        known, turn = min(2 * known, half), turn + 1
+    send_in(last, done + 1, half)
+    send_in(0, done + 1, half)
+    for k in range(chunks):
+        land1[k, me] = xs[me * chunks + k]
+    ywin[:, 0:8, :] = jnp.zeros((2, 8, m), F32)
     get_cs.wait()
     synthesize(last)
     tail = pltpu.make_async_remote_copy(
@@ -148,12 +182,10 @@
     def _():
         tail.start()
 
-    def send_rest(k, c):
-        send_in(k)
-        return c
-
-    lax.fori_loop(1, last, send_rest, 0)
-    get_rs.wait()
+    for k in range(1, last):
+        send_in(k, done + 1, half)
+    for copy in (get_rs, get_st, get_at):
+        copy.wait()
 
     def resampled(k):
         @pl.when(k == 0)
@@ -219,7 +251,7 @@
         out = product((cs[0], cs[1]), split(u2[...]), ((1,), (1,)))
         sbuf[p] = out.reshape(n, cb, L)
         land2[p, me] = sbuf[p, me]
-        send_to_all(lambda dev: sbuf.at[p, dev], land2.at[p, me], send2.at[p], recv2.at[p])
+        send_to(lambda dev: sbuf.at[p, dev], land2.at[p, me], send2.at[p], recv2.at[p], 1, nc // 2)
 
     def step(p, c):
         @pl.when(p < last)
@@ -243,19 +275,28 @@
         wait_bytes(land1.at[k], send1.at[k])
     for p in range(pieces):
         wait_bytes(land2.at[p], recv2.at[p])
-
-    def place(t, c):
-        for u in range(pieces):
-            a = land2[(2 * u) % pieces, 2 * t + (2 * u) // pieces]
-            b = land2[(2 * u + 1) % pieces, 2 * t + (2 * u + 1) // pieces]
-            lanes = pl.ds(pl.multiple_of(t * (pieces * L) + u * L, L), L)
-            o_ref[0, :, lanes] = jnp.where(low, a, pltpu.roll(b, W, 1))
-            o_ref[1, :, lanes] = jnp.where(low, pltpu.roll(a, W, 1), b)
-        return c
-
-    lax.fori_loop(0, n // 2, place, 0)
+        pairs = [(u, divmod(2 * u, pieces), divmod(2 * u + 1, pieces)) for u in range(pieces)]
+        pairs = [pair for pair in pairs if max(pair[1][1], pair[2][1]) == p]
+
+        def place(t, c, pairs=pairs):
+            for u, (da, pa), (db, pb) in pairs:
+                a = land2[pa, 2 * t + da]
+                b = land2[pb, 2 * t + db]
+                first = 2 * (t * pieces + u)
+                o_ref[pl.ds(first, cb, stride=out_rows), :] = jnp.where(low, a, pltpu.roll(b, W, 1))
+                o_ref[pl.ds(first + 1, cb, stride=out_rows), :] = jnp.where(low, pltpu.roll(a, W, 1), b)
+            return c
+
+        if pairs:
+            lax.fori_loop(0, n // 2, place, 0)
+
     for p in range(pieces):
         wait_bytes(land2.at[p], send2.at[p])
+
+
+def rows_of(spectra):
+    parts = spectra.reshape(spectra.shape[0], 2, -1, L)
+    return jnp.swapaxes(parts, 1, 2).reshape(-1, L)
 
 
 def shards(n, spectra, synth_taps, analysis_taps):
@@ -266,15 +307,19 @@
     pieces = UP * own // DOWN // W
     wide = UP * m // DOWN // L
     blocks = m // L
+    pin = lambda a: pltpu.with_memory_space_constraint(a, pltpu.HBM)
     vmem = pl.BlockSpec(memory_space=pltpu.VMEM)
     hbm = pl.BlockSpec(memory_space=pl.ANY)
     dma = pltpu.SemaphoreType.DMA
     out = pl.pallas_call(
         functools.partial(kernel, n),
-        out_shape=jax.ShapeDtypeStruct((2, cb, UP * frames // DOWN), F32),
-        in_specs=[vmem, vmem, vmem, hbm, hbm],
+        out_shape=jax.ShapeDtypeStruct((cb * 2 * UP * frames // DOWN // L, L), F32),
+        in_specs=[hbm] * 5,
         out_specs=vmem,
         scratch_shapes=[
+            pltpu.VMEM((cb * (2 * frames // L + 8), L), F32),
+            pltpu.VMEM(synth_taps.shape, F32),
+            pltpu.VMEM(analysis_taps.shape, F32),
             pltpu.VMEM((2, m, 2 * m), jnp.bfloat16),
             pltpu.VMEM((2, m + L, wide * L), jnp.bfloat16),
             pltpu.VMEM((n * chunks, cb, L), F32),
@@ -289,16 +334,17 @@
             pltpu.VMEM((2 * W, 2 * m), F32),
             pltpu.VMEM((pieces, n, cb, L), F32),
             pltpu.VMEM((pieces, n, cb, L), F32),
-            dma, dma, dma((chunks,)), dma((chunks,)), dma, dma, dma((pieces,)), dma((pieces,)),
+            dma((cb,)), dma, dma, dma, dma, dma((chunks,)), dma((chunks,)), dma, dma, dma((pieces,)), dma((pieces,)),
+            pltpu.SemaphoreType.REGULAR((8,)),
         ],
         compiler_params=pltpu.CompilerParams(
             collective_id=0, has_side_effects=True, vmem_limit_bytes=40 << 20
         ),
     )(
-        jnp.swapaxes(spectra, 0, 1), synth_taps, analysis_taps,
-        halves(dft_table(m)), halves(resample_table(m)),
+        pin(rows_of(spectra)), pin(synth_taps), pin(analysis_taps),
+        pin(halves(dft_table(m))), pin(halves(resample_table(m))),
     )
-    return jnp.swapaxes(out, 0, 1)
+    return jnp.swapaxes(out.reshape(cb, -1, 2, L), 1, 2).reshape(cb, 2, -1)
 
 
 def solution(mesh):

time: 250 us -> 242 us (0.968)
  local copies, waits for them, and re-layouts: 7 us -> 1.06 us
    unnamed x9 -> x1, local copies, waits for them, and re-layouts: 4.93 us -> 1.06 us
where the time goes in v2:
time: 242 us
  Pallas kernels  241 us (100%)
    pallas_call x1, Pallas kernels, shards(): pl.pallas_call(functools.partial(kernel, n), out_shape=jax.ShapeDtypeStru...  241 us

profile of v2, /device:TPU:37, one launch (start us, length us, event | category | flops | bytes accessed | tf_op | source)
XLA Modules:
  0.0 242.2 jit_solution(3827619311281102490)
XLA Ops:
  0.0 241.1 %shard_map.55 = f32[2560,128]{1,0:T(8,128)S(1)} custom-call(f32[2048,128]{1,0:T(8,128)} %bitcast.11, f32[16,512]{1,0:T(8,128)} %st_hbm.1, f32[16,512]{1,0:T(8,128)} %at_hbm.1, bf16[2,512,1024]{2,1,0:T(8,128)(2,1)} %constant.4.clone.cs_hbm, bf16[2,640,640]{2,1,0:T(8,128)(2,1)} %constant.5.clone.rs_hbm), custom_call_target="tpu_custom_call" | custom-call | tf_op jit(solution)/shard_map/pallas_call | solution.py:314
  241.1 1.1 copy.9

commit v3 on v2

--- a/solution.py
+++ b/solution.py
@@ -12,7 +12,7 @@
 RT = 32
 PHASES = 64
 UP, DOWN = 5, 4
-REACH = 4
+REACH = 8
 W = 64
 L = 128
 HALO = 32

time: 242 us -> 238 us (0.983)
  Pallas kernels: 241 us -> 237 us
    pallas_call x1, Pallas kernels: 241 us -> 237 us  [shards(): pl.pallas_call(functools.partial(kernel, n), out_shape=jax.ShapeDtypeStru...]
where the time goes in v3:
time: 238 us
  Pallas kernels  237 us (100%)
    pallas_call x1, Pallas kernels, shards(): pl.pallas_call(functools.partial(kernel, n), out_shape=jax.ShapeDtypeStru...  237 us

profile of v3, /device:TPU:37, one launch (start us, length us, event | category | flops | bytes accessed | tf_op | source)
XLA Modules:
  0.0 238.4 jit_solution(14243954786801841614)
XLA Ops:
  0.0 237.3 %shard_map.55 = f32[2560,128]{1,0:T(8,128)S(1)} custom-call(f32[2048,128]{1,0:T(8,128)} %bitcast.11, f32[16,512]{1,0:T(8,128)} %st_hbm.1, f32[16,512]{1,0:T(8,128)} %at_hbm.1, bf16[2,512,1024]{2,1,0:T(8,128)(2,1)} %constant.4.clone.cs_hbm, bf16[2,640,640]{2,1,0:T(8,128)(2,1)} %constant.5.clone.rs_hbm), custom_call_target="tpu_custom_call" | custom-call | tf_op jit(solution)/shard_map/pallas_call | solution.py:314
  237.3 1.1 copy.9

commit v4 on v3

--- a/solution.py
+++ b/solution.py
@@ -125,7 +125,7 @@
 
         def step(j, c):
             d = far - j // 4
-            sign = 1 - 2 * (j // 2 % 2)
+            sign = 1 - 2 * ((j // 2 + core) % 2)
 
             @pl.when(jnp.logical_not(jnp.logical_and(2 * d == nc, sign == -1)))
             def _():
@@ -156,17 +156,19 @@
         copy.wait()
     lax.fori_loop(0, n // 2, arrange, 0)
     pl.semaphore_wait(barrier, met)
-    known, turn, done = reach, 0, 0
+    known, turn = reach, 0
+    done = [0] * chunks
     while known < half:
         for offset in (known, -known):
             signal(ready.at[turn], at(offset, core))
-        for k in range(chunks):
-            send_in((k - 1) % chunks, done + 1, known)
-        done = known
+        for k in (last, *range(last)):
+            if 2 * known < half or k in (last, 0):
+                send_in(k, done[k] + 1, known)
+                done[k] = known
         pl.semaphore_wait(ready.at[turn], 2)
         known, turn = min(2 * known, half), turn + 1
-    send_in(last, done + 1, half)
-    send_in(0, done + 1, half)
+    send_in(last, done[last] + 1, half)
+    send_in(0, done[0] + 1, half)
     for k in range(chunks):
         land1[k, me] = xs[me * chunks + k]
     ywin[:, 0:8, :] = jnp.zeros((2, 8, m), F32)
@@ -183,7 +185,7 @@
         tail.start()
 
     for k in range(1, last):
-        send_in(k, done + 1, half)
+        send_in(k, done[k] + 1, half)
     for copy in (get_rs, get_st, get_at):
         copy.wait()
 

time: 238 us -> 239 us (level)
  no operation moved by 1% of the time
where the time goes in v4:
time: 239 us
  Pallas kernels  238 us (100%)
    pallas_call x1, Pallas kernels, shards(): pl.pallas_call(functools.partial(kernel, n), out_shape=jax.ShapeDtypeStru...  238 us

profile of v4, /device:TPU:37, one launch (start us, length us, event | category | flops | bytes accessed | tf_op | source)
XLA Modules:
  0.0 239.1 jit_solution(11716324022508635987)
XLA Ops:
  0.0 238.0 %shard_map.55 = f32[2560,128]{1,0:T(8,128)S(1)} custom-call(f32[2048,128]{1,0:T(8,128)} %bitcast.11, f32[16,512]{1,0:T(8,128)} %st_hbm.1, f32[16,512]{1,0:T(8,128)} %at_hbm.1, bf16[2,512,1024]{2,1,0:T(8,128)(2,1)} %constant.4.clone.cs_hbm, bf16[2,640,640]{2,1,0:T(8,128)(2,1)} %constant.5.clone.rs_hbm), custom_call_target="tpu_custom_call" | custom-call | tf_op jit(solution)/shard_map/pallas_call | solution.py:316
  238.0 1.1 copy.9
